TPU v7x, 256 devices: a whole 4x4x8 slice. The times are simulated.
256 devices in a mesh: seq: 32 (over z, x_hi, core), exp: 8 (over x_lo, y).
Axes of the slice: x: 4 (x_hi: 2, x_lo: 2; x = x_hi * 2 + x_lo), y: 4, z: 8, core: 2. Of those that a mesh axis runs over, the one named last changes fastest.
Arguments:
- queries: bfloat16 [3072, 4096], P('seq', 'exp'), may hold values from -17 to 17
- keys: bfloat16 [3072, 1024], P('seq', 'exp'), may hold values from -17 to 17
- values: bfloat16 [3072, 1024], P('seq', 'exp'), may hold values from -6 to 6
- residual: bfloat16 [3072, 4096], P('seq', 'exp'), may hold values from -48 to 48
- norm_gain: float32 [4096], P('exp'), may hold values from 0.1 to 1.9
- routes: int32 [3072, 2], P('seq'), may hold values from 0 to 7, all different within a row; in each aligned block of 96 rows (0 to 95, 96 to 191, ...) at most 36 rows name the same one
- gates: float32 [3072, 2], P('seq'), may hold values from 0.1 to 0.9
- w_gate: bfloat16 [8, 4096, 14336], P('exp', None, 'seq'), may hold values from -0.09375 to 0.09375
- w_up: bfloat16 [8, 4096, 14336], P('exp', None, 'seq'), may hold values from -0.09375 to 0.09375
- w_down: bfloat16 [8, 14336, 4096], P('exp', 'seq'), may hold values from -0.046875 to 0.046875
Outputs:
- attended: bfloat16 [3072, 4096], P('seq', 'exp')
- layer_out: bfloat16 [3072, 4096], P('seq', 'exp')
Inputs may be any that keep to these rules, and one draw needn't show every extreme that they name: `routes`: each row names 2 different experts. In the rows of one device no expert is named more than 36 times, a bound that some block reaches.
All inputs are finite; a program needn't handle non-finite values.
Results may differ from a plain program's by a relative error of at most 0.0075.
Values may be sent and summed in bfloat16 or wider, within the bound.
A program may use at most 128 MiB of HBM per device.

v0:
```python
import math

import jax
import jax.numpy as jnp
from jax import lax
from jax.sharding import PartitionSpec as P

D = 4096
QUERY_HEADS = 32
KEY_VALUE_HEADS = 8
HEAD_WIDTH = 128
TOP = 2


def sent_together(arrays, axis, dim, along):
    both = jnp.concatenate(arrays, axis=along)
    filled, at, outs = (lax.all_gather(both, axis, axis=dim, tiled=True), 0, [])
    for a in arrays:
        outs.append(lax.slice_in_dim(filled, at, at + a.shape[along], axis=along))
        at += a.shape[along]
    return tuple(outs)


def sent_to_all(value, axis):
    peers = lax.axis_size(axis)
    return lax.all_to_all(
        jnp.broadcast_to(value[None], (peers, *value.shape)), axis, 0, 0, tiled=True
    )


def over_copies(value, axis):
    everything = sent_to_all(value, axis)
    return jnp.sum(everything, axis=0)


def shards(queries, keys, values, residual, norm_gain, routes, gates, w_gate, w_up, w_down):
    tok_rows = queries.shape[0]
    local_width = queries.shape[1]
    local_heads = keys.shape[1] // HEAD_WIDTH
    group_width = QUERY_HEADS // KEY_VALUE_HEADS
    exp_count = lax.axis_size("exp")
    score_scale = 1.0 / math.sqrt(HEAD_WIDTH)
    first_pos = lax.axis_index("seq") * tok_rows
    query_pos = first_pos + jnp.arange(tok_rows, dtype=jnp.int32)
    query_grouped = queries.reshape(tok_rows, local_heads, group_width, HEAD_WIDTH)
    running_max = jnp.full((local_heads, group_width, tok_rows), -1e30, jnp.float32)
    key_block, value_block = sent_together((keys, values), "seq", 0, 1)
    length = key_block.shape[0]
    key_piece = key_block.reshape(length, local_heads, HEAD_WIDTH)
    value_piece = value_block.reshape(length, local_heads, HEAD_WIDTH)
    scores = (
        jnp.einsum("tkgd,pkd->kgtp", query_grouped, key_piece, preferred_element_type=jnp.float32)
        * score_scale
    )
    key_pos = jnp.arange(length, dtype=jnp.int32)
    causal_mask = key_pos[None, :] <= query_pos[:, None]
    scores = jnp.where(causal_mask, scores, -1e30)
    new_max = jnp.maximum(running_max, jnp.max(scores, axis=-1))
    exp_terms = jnp.where(causal_mask, jnp.exp(scores - new_max[..., None]), 0.0)
    new_sum = jnp.sum(exp_terms, axis=-1)
    new_weighted = jnp.einsum(
        "kgtp,pkd->kgtd",
        exp_terms.astype(jnp.bfloat16),
        value_piece,
        preferred_element_type=jnp.float32,
    )
    attn = new_weighted / new_sum[..., None]
    attn = jnp.transpose(attn, (2, 0, 1, 3)).reshape(tok_rows, local_width)
    attended = (residual.astype(jnp.float32) + attn).astype(jnp.bfloat16)
    stream = attended.astype(jnp.float32)
    square_total = over_copies(jnp.sum(stream * stream, axis=1), "exp")
    normed = (stream * lax.rsqrt(square_total[:, None] / D + 1e-05) * norm_gain[None, :]).astype(
        jnp.bfloat16
    )
    experts = exp_count * w_gate.shape[0]
    capacity = min(tok_rows, 3 * TOP * tok_rows // (2 * experts))
    expert_ids = routes.reshape(tok_rows * TOP)
    one_hot = (expert_ids[:, None] == jnp.arange(experts, dtype=jnp.int32)[None, :]).astype(
        jnp.int32
    )
    before = jnp.cumsum(one_hot, axis=0) - one_hot
    slot_index = jnp.sum(before * one_hot, axis=1)
    dest_slot = expert_ids * capacity + slot_index
    slot_match = (
        dest_slot[:, None] == jnp.arange(experts * capacity, dtype=jnp.int32)[None, :]
    ).astype(jnp.float32)
    dispatch = jnp.sum(jnp.transpose(slot_match).reshape(experts * capacity, tok_rows, TOP), axis=2)
    outgoing = jnp.dot(
        dispatch.astype(jnp.bfloat16), normed, preferred_element_type=jnp.float32
    ).astype(jnp.bfloat16)
    outgoing = outgoing.reshape(experts, capacity, local_width)
    gate_mat = w_gate[0]
    up_mat = w_up[0]
    down_mat = w_down[0]
    arrived = lax.all_to_all(outgoing, "exp", split_axis=0, concat_axis=2, tiled=True)
    local_rows = arrived.reshape(capacity, D)
    flat_rows = lax.all_gather(local_rows, "seq", axis=0, tiled=True)
    hidden = (
        jax.nn.silu(jnp.dot(flat_rows, gate_mat, preferred_element_type=jnp.float32))
        * jnp.dot(flat_rows, up_mat, preferred_element_type=jnp.float32)
    ).astype(jnp.bfloat16)
    summed = lax.psum_scatter(
        jnp.dot(hidden, down_mat, preferred_element_type=jnp.float32).astype(jnp.bfloat16),
        "seq",
        scatter_dimension=0,
        tiled=True,
    )
    expert_out = summed.reshape(1, capacity, exp_count, local_width)
    returned = lax.all_to_all(expert_out, "exp", split_axis=2, concat_axis=0, tiled=True)
    returned_rows = returned.reshape(experts * capacity, local_width)
    weighted_match = slot_match * gates.reshape(tok_rows * TOP)[:, None]
    mixing = jnp.sum(weighted_match.reshape(tok_rows, TOP, experts * capacity), axis=1)
    expert_mix = jnp.dot(mixing, returned_rows.astype(jnp.float32))
    layer_out = (stream + expert_mix).astype(jnp.bfloat16)
    return (attended, layer_out)


def solution(mesh):
    in_specs = (
        P("seq", "exp"),
        P("seq", "exp"),
        P("seq", "exp"),
        P("seq", "exp"),
        P("exp"),
        P("seq", None),
        P("seq", None),
        P("exp", None, "seq"),
        P("exp", None, "seq"),
        P("exp", "seq", None),
    )
    out_specs = (P("seq", "exp"), P("seq", "exp"))
    return jax.shard_map(shards, mesh=mesh, in_specs=in_specs, out_specs=out_specs, check_vma=False)
```

profile of v0, /device:TPU:13, one launch (start us, length us, event | category | flops | bytes accessed | tf_op | source)
XLA Modules:
  0.0 427.0 jit_solution(4100689388805581193)
XLA Ops:
  7.2 1.4 pad_maximum_fusion
  11.7 79.2 %all-gather.4.cloned.1.call-done = bf16[3072,256]{1,0:T(8,128)(2,1)} async-done(((bf16[96,256]{1,0:T(8,128)(2,1)}), bf16[3072,256]{1,0:T(8,128)(2,1)}) %all-gather.4.cloned.1.call-update) | async-done | bytes 1572880 | tf_op jit(solution)/shard_map/all_gather | solution.py:17
  90.9 2.2 fusion.50
  93.1 1.1 fusion.1
  94.5 1.0 fusion.31
  96.4 5.8 %all-to-all-start = ((f32[8,1,96]{2,1,0:T(1,128)}), f32[8,1,96]{2,1,0:T(1,128)S(1)}, u32[]{:S(2)}, u32[]{:S(2)}) async-start(f32[8,1,96]{2,1,0:T(1,128)} %broadcast_in_dim.34), calls=%async_computation | async-start | bytes 8192 | tf_op jit(solution)/shard_map/all_to_all | solution.py:26
  102.2 3.7 all-to-all-done
  106.3 9.1 %all_to_all.36 = bf16[8,36,512]{2,1,0:T(8,128)(2,1)S(1)} all-to-all(bf16[8,36,512]{2,1,0:T(8,128)(2,1)S(1)} %reshape.123), channel_id=1, replica_groups=mesh['seq'=32,'exp'=8] {'exp'}, dimensions={0} | all-to-all | bytes 589824 | tf_op jit(solution)/shard_map/all_to_all | solution.py:95
  115.6 0.9 reshape.128
  116.5 105.8 %all-gather.6.cloned.1.call-done = bf16[32,36,4096]{2,1,0:T(8,128)(2,1)} async-done(((bf16[1,36,4096]{2,1,0:T(8,128)(2,1)}), bf16[32,36,4096]{2,1,0:T(8,128)(2,1)}) %all-gather.6.cloned.1.call-update) | async-done | bytes 9437200 | tf_op jit(solution)/shard_map/all_gather | solution.py:97
  222.3 13.2 %reshape.129 = bf16[1152,4096]{1,0:T(8,128)(2,1)} reshape(bf16[32,36,4096]{2,1,0:T(8,128)(2,1)} %all-gather.6.cloned.1.call-done) | data formatting | bytes 18874368
  235.5 9.7 %fusion.6 = f32[1152,448]{0,1:T(8,128)S(1)} fusion(bf16[1152,4096]{1,0:T(8,128)(2,1)} %reshape.129, bf16[1,4096,448]{1,2,0:T(8,128)(2,1)} %param.17), kind=kOutput, calls=%fused_computation.8 | convolution fusion | flops 4227858432 | bytes 15171584 | tf_op jit(solution)/shard_map/dot_general | solution.py:99
  245.2 17.4 %convolution_convert_fusion = bf16[1152,4096]{1,0:T(8,128)(2,1)} fusion(bf16[1,448,4096]{2,1,0:T(8,128)(2,1)} %param.19, bf16[1152,4096]{1,0:T(8,128)(2,1)} %reshape.129, bf16[1,4096,448]{1,2,0:T(8,128)(2,1)} %param.18, f32[1152,448]{0,1:T(8,128)S(1)} %fusion.6), kind=kOutput, calls=%fused_computation | convolution fusion | flops 8463532032 | bytes 28278784 | tf_op jit(solution)/shard_map/dot_general | solution.py:103
  262.6 116.6 %fusion = bf16[40,4096]{1,0:T(8,128)(2,1)S(1)} fusion(bf16[1152,4096]{1,0:T(8,128)(2,1)} %convolution_convert_fusion), kind=kCustom, calls=%all-reduce-scatter | all-reduce-scatter fusion | flops 5242881 | bytes 9765888
  379.2 4.6 %collective-permute-start = (bf16[40,4096]{1,0:T(8,128)(2,1)S(1)}, bf16[40,4096]{1,0:T(8,128)(2,1)S(1)}, u32[]{:S(2)}, u32[]{:S(2)}) collective-permute-start(bf16[40,4096]{1,0:T(8,128)(2,1)S(1)} %fusion), channel_id=1, source_target_pairs={{0,8},{8,16},{16,24},{24,32},{32,40},{40,48},{48,56},{56,64},{64,7... | collective-permute-start | bytes 983048
  383.8 9.7 %collective-permute-start.1 = (bf16[40,4096]{1,0:T(8,128)(2,1)S(1)}, bf16[40,4096]{1,0:T(8,128)(2,1)S(1)}, u32[]{:S(2)}, u32[]{:S(2)}) collective-permute-start(bf16[40,4096]{1,0:T(8,128)(2,1)S(1)} %fusion), channel_id=1, source_target_pairs={{0,16},{8,24},{16,32},{24,40},{32,48},{40,56},{48,64},{56,72},{64,... | collective-permute-start | bytes 983048
  393.5 1.9 collective-permute-start.2
  395.5 3.7 collective-permute-start.3
  400.5 5.3 %collective-permute-done.3 = bf16[4,4096]{1,0:T(4,128)(2,1)S(1)} collective-permute-done((bf16[4,4096]{1,0:T(4,128)(2,1)S(1)}, bf16[4,4096]{1,0:T(4,128)(2,1)S(1)}, u32[]{:S(2)}, u32[]{:S(2)}) %collective-permute-start.3) | collective-permute-done | bytes 32800
  405.8 1.7 concatenate.4
  407.7 0.8 copy.57
  408.5 4.7 %all-to-all-start.2 = ((bf16[1,36,8,512]{3,1,0,2:T(8,128)(2,1)}), bf16[1,36,8,512]{3,1,0,2:T(8,128)(2,1)S(1)}, u32[]{:S(2)}, u32[]{:S(2)}) async-start(bf16[1,36,8,512]{3,1,0,2:T(8,128)(2,1)} %copy.57), calls=%async_computation.2 | async-start | bytes 655360 | tf_op jit(solution)/shard_map/all_to_all | solution.py:109
  413.3 6.0 %all-to-all-done.2 = bf16[1,36,8,512]{3,1,0,2:T(8,128)(2,1)S(1)} async-done(((bf16[1,36,8,512]{3,1,0,2:T(8,128)(2,1)}), bf16[1,36,8,512]{3,1,0,2:T(8,128)(2,1)S(1)}, u32[]{:S(2)}, u32[]{:S(2)}) %all-to-all-start.2) | async-done | bytes 294944 | tf_op jit(solution)/shard_map/all_to_all | solution.py:109
  419.3 0.9 fusion.27
  (53 shorter events, 5.7 us)
Async XLA Ops:
  7.2 83.7 %copy-start = (bf16[96,512]{1,0:T(8,128)(2,1)S(1)}, bf16[96,512]{1,0:T(8,128)(2,1)}, u32[]{:S(2)}) copy-start(bf16[96,512]{1,0:T(8,128)(2,1)} %param.10) | copy-start | bytes 294916
  7.2 83.7 %all-gather.4.cloned.1.call-start = ((), (), s32[]{:S(2)}) async-start(), calls=%async_computation.3 | async-start | bytes 1622016 | tf_op jit(solution)/shard_map/all_gather | solution.py:17
  93.1 1.4 copy-start.6
  94.5 1.1 copy-start.2
  94.5 11.4 %copy-start.3 = (f32[512]{0:T(512)S(1)}, f32[512]{0:T(512)}, u32[]{:S(2)}) copy-start(f32[512]{0:T(512)} %param.14) | copy-start | bytes 6148
  95.8 323.6 %copy-start.1 = (bf16[96,512]{1,0:T(8,128)(2,1)}, bf16[96,512]{1,0:T(8,128)(2,1)S(1)}, u32[]{:S(2)}) copy-start(bf16[96,512]{1,0:T(8,128)(2,1)S(1)} %get-tuple-element.3) | copy-start | bytes 294916
  96.4 9.5 %all-to-all-start = ((f32[8,1,96]{2,1,0:T(1,128)}), f32[8,1,96]{2,1,0:T(1,128)S(1)}, u32[]{:S(2)}, u32[]{:S(2)}) async-start(f32[8,1,96]{2,1,0:T(1,128)} %broadcast_in_dim.34), calls=%async_computation | async-start | bytes 8192 | tf_op jit(solution)/shard_map/all_to_all | solution.py:26
  102.1 120.1 %all-gather.6.cloned.1.call-start = ((), (), s32[]{:S(2)}) async-start(), calls=%async_computation.4 | async-start | bytes 10813440 | tf_op jit(solution)/shard_map/all_gather | solution.py:97
  262.6 136.6 %copy-start.5 = (u32[256]{0:T(256)S(1)}, u32[256]{0:T(256)}, u32[]{:S(2)}) copy-start(u32[256]{0:T(256)} %constant.43) | copy-start | bytes 3076
  379.2 34.0 %copy-start.4 = (f32[96,2]{0,1:T(2,128)S(1)}, f32[96,2]{0,1:T(2,128)}, u32[]{:S(2)}) copy-start(f32[96,2]{0,1:T(2,128)} %param.16) | copy-start | bytes 2308
  379.2 26.6 %collective-permute-start = (bf16[40,4096]{1,0:T(8,128)(2,1)S(1)}, bf16[40,4096]{1,0:T(8,128)(2,1)S(1)}, u32[]{:S(2)}, u32[]{:S(2)}) collective-permute-start(bf16[40,4096]{1,0:T(8,128)(2,1)S(1)} %fusion), channel_id=1, source_target_pairs={{0,8},{8,16},{16,24},{24,32},{32,40},{40,48},{48,56},{56,64},{64,7... | collective-permute-start | bytes 983048
  383.8 22.0 %collective-permute-start.1 = (bf16[40,4096]{1,0:T(8,128)(2,1)S(1)}, bf16[40,4096]{1,0:T(8,128)(2,1)S(1)}, u32[]{:S(2)}, u32[]{:S(2)}) collective-permute-start(bf16[40,4096]{1,0:T(8,128)(2,1)S(1)} %fusion), channel_id=1, source_target_pairs={{0,16},{8,24},{16,32},{24,40},{32,48},{40,56},{48,64},{56,72},{64,... | collective-permute-start | bytes 983048
  393.5 12.2 %collective-permute-start.2 = (bf16[40,4096]{1,0:T(8,128)(2,1)S(1)}, bf16[40,4096]{1,0:T(8,128)(2,1)S(1)}, u32[]{:S(2)}, u32[]{:S(2)}) collective-permute-start(bf16[40,4096]{1,0:T(8,128)(2,1)S(1)} %fusion), channel_id=1, source_target_pairs={{0,24},{8,32},{16,40},{24,48},{32,56},{40,64},{48,72},{56,80},{64,... | collective-permute-start | bytes 983048
  395.5 10.3 %collective-permute-start.3 = (bf16[4,4096]{1,0:T(4,128)(2,1)S(1)}, bf16[4,4096]{1,0:T(4,128)(2,1)S(1)}, u32[]{:S(2)}, u32[]{:S(2)}) collective-permute-start(bf16[4,4096]{1,0:T(4,128)(2,1)S(1)} %slice.24), channel_id=1, source_target_pairs={{0,32},{8,40},{16,48},{24,56},{32,64},{40,72},{48,80},{56,88},{64,... | collective-permute-start | bytes 98312
  408.5 10.8 %all-to-all-start.2 = ((bf16[1,36,8,512]{3,1,0,2:T(8,128)(2,1)}), bf16[1,36,8,512]{3,1,0,2:T(8,128)(2,1)S(1)}, u32[]{:S(2)}, u32[]{:S(2)}) async-start(bf16[1,36,8,512]{3,1,0,2:T(8,128)(2,1)} %copy.57), calls=%async_computation.2 | async-start | bytes 655360 | tf_op jit(solution)/shard_map/all_to_all | solution.py:109
Sparse Core Ops, SparseCore 0:
  11.3 79.5 all-gather.3
  116.6 105.6 all-gather.5
where the time goes:
time: 432 us; the launch traced here: 427 us
  waiting for transfers between devices  200 us (46%)
  blocking collectives  126 us (29%)
  matrix products  31.4 us (7%)
  starting transfers between devices  30.5 us (7%)
  local copies, waits for them, and re-layouts  20 us (5%)
  between operations  14.9 us (3%)
  other arithmetic  4.52 us (1%)
    unnamed x1, blocking collectives  117 us
    all_gather x1, waiting for transfers between devices, shards(): flat_rows = lax.all_gather(local_rows, 'seq', axis=0, tiled=True)  106 us
    all_gather x1, waiting for transfers between devices, sent_together(): filled, at, outs = (lax.all_gather(both, axis, axis=dim, tiled=True), 0, [])  79.2 us
    unnamed x4, starting transfers between devices  20 us
    unnamed x22, local copies, waits for them, and re-layouts  17.6 us
    dot_general x1, matrix products, shards(): jnp.dot(hidden, down_mat, preferred_element_type=jnp.float32)  17.4 us
    dot_general x1, matrix products, shards(): jnp.dot(flat_rows, gate_mat, preferred_element_type=jnp.float32)  9.65 us
    all_to_all x1, blocking collectives, shards(): lax.all_to_all(outgoing, 'exp', split_axis=0, concat_axis=2, tiled=True)  9.13 us
  transfers between devices with their start and end apart: 8, of which 5 were waited for; matrix products, arithmetic and copies ran while one was open for 1% of the time, Pallas kernels for 0%

commit v1 on v0

v1 whole, which is shorter than its diff:
```python
import functools
import math

import jax
import jax.numpy as jnp
from jax import lax
from jax.experimental import pallas as pl
from jax.experimental.pallas import tpu as pltpu
from jax.sharding import PartitionSpec as P

D = 4096
HEAD_WIDTH = 128
GROUP = 4
TOK = 96
EXPERTS = 8
CAP = 36
PITCH = 48
PLANE = 4
ROWS = PLANE * CAP
WIDE = 512
FF_LOCAL = 448
MESH = pl.DeviceIdType.MESH
F32 = jnp.float32
BF16 = jnp.bfloat16


class Place:
    def __init__(self, depth):
        self.depth = depth
        self.half = depth // 2
        self.seq = lax.axis_index("seq")
        self.exp = lax.axis_index("exp")
        self.z = self.seq // PLANE
        self.j = lax.rem(self.seq, PLANE)
        xh, c = self.j // 2, lax.rem(self.j, 2)
        self.jp = (1 - xh) * 2 + c
        self.jc = xh * 2 + (1 - c)
        self.jcp = (1 - xh) * 2 + (1 - c)
        self.up = self.at(lax.rem(self.z + 1, depth), self.j)
        self.down = self.at(lax.rem(self.z + depth - 1, depth), self.j)
        self.partner = self.at(self.z, self.jp)
        self.sibling = self.at(self.z, self.jc)

    def at(self, z, j, e=None):
        return {"seq": z * PLANE + j, "exp": self.exp if e is None else e}


def remote(src, dst, send_sem, recv_sem, device):
    return pltpu.make_async_remote_copy(
        src_ref=src, dst_ref=dst, send_sem=send_sem, recv_sem=recv_sem,
        device_id=device, device_id_type=MESH,
    )


class Gather:
    def __init__(self, place, unit, half, sems):
        self.p, self.unit, self.cut = place, unit, half
        self.zs, self.zr, self.xs, self.xr, self.ds, self.dr = sems
        self.sent = []

    def send(self, ref, ss, rs, device):
        cp = remote(ref, ref, ss, rs, device)
        cp.start()
        self.sent.append(cp)

    def got(self, ref, rs):
        remote(ref, ref, self.zs.at[0, 0], rs, self.p.up).wait_recv()

    def ring(self, src_slot, plus, d, k, j, u):
        h = self.p.half
        sem = 2 * (d + 1) - 1 if plus else 2 * (d + 1)
        dst_slot = min(sem, 2 * h - 1)
        src, dst = self.unit(src_slot, j, u), self.unit(dst_slot, j, u)
        if d + 1 == h:
            src, dst = self.cut(src, 0 if plus else 1), self.cut(dst, 0 if plus else 1)
        cp = remote(src, dst, self.zs.at[sem, k], self.zr.at[sem, k], self.p.up if plus else self.p.down)
        cp.start()
        self.sent.append(cp)

    def across(self, slot, k, j, u):
        self.send(self.unit(slot, j, u), self.ds.at[slot, k], self.dr.at[slot, k], self.p.sibling)

    def start(self):
        p = self.p
        self.send(self.unit(0, p.j, 0), self.xs.at[8], self.xr.at[8], p.partner)
        for u in (1, 0):
            self.ring(0, True, 0, u, p.j, u)
            self.ring(0, False, 0, u, p.j, u)
        self.send(self.unit(0, p.j, 1), self.xs.at[0], self.xr.at[0], p.partner)
        self.across(0, 0, p.j, 0)
        self.across(0, 1, p.j, 1)

    def start_partner(self):
        p = self.p
        self.got(self.unit(0, p.jp, 0), self.xr.at[8])
        self.ring(0, True, 0, 2, p.jp, 0)
        self.ring(0, False, 0, 2, p.jp, 0)
        self.across(0, 2, p.jp, 0)

    def arrive(self, d):
        p, h = self.p, self.p.half
        for k, own, u in ((1, True, 1), (0, True, 0), (2, False, 0)):
            j = p.j if own else p.jp
            if d < h:
                for plus in (True, False):
                    slot = 2 * d - 1 if plus else 2 * d
                    self.got(self.unit(slot, j, u), self.zr.at[slot, k])
                    self.ring(slot, plus, d, k, j, u)
                slots = (2 * d - 1, 2 * d)
            else:
                slot = 2 * h - 1
                for part in (0, 1):
                    self.got(self.cut(self.unit(slot, j, u), part), self.zr.at[slot + part, k])
                slots = (slot,)
            for slot in slots:
                if k == 1:
                    self.send(self.unit(slot, j, 1), self.xs.at[slot], self.xr.at[slot], p.partner)
                self.across(slot, k, j, u)

    def arrive_partner(self, slots):
        for slot in slots:
            self.got(self.unit(slot, self.p.jp, 1), self.xr.at[slot])
            self.across(slot, 3, self.p.jp, 1)

    def arrive_sibling(self, slots):
        p = self.p
        for slot in slots:
            for k, (j, u) in enumerate(((p.jc, 0), (p.jc, 1), (p.jcp, 0), (p.jcp, 1))):
                self.got(self.unit(slot, j, u), self.dr.at[slot, k])

    def finish(self):
        for cp in self.sent:
            cp.wait_send()


def slots_of(d, half):
    if d == 0:
        return (0,)
    return (2 * d - 1, 2 * d) if d < half else (2 * half - 1,)


def kernel(
    depth,
    q_hbm, k_hbm, v_hbm, res_hbm, gain_hbm, routes_hbm, gates_hbm, wg_hbm, wu_hbm, wd_hbm,
    att_hbm, out_hbm,
    q_in, res_in, gain_in, routes_in, gates_in, wg, wu, wd,
    kg, vg, qs, m_s, l_s, acc_s, att, ss_buf, outgoing, rx, xg, hb, yb, dr_buf, zr_buf, xr_buf, fb, rb, ret, mixed, out_v,
    load_sem, store_sem, g_zs, g_xs, g_ds, a_zr, a_xr, a_dr, b_zr, b_xr, b_dr,
    ss_s, ss_r, x_s, x_r, c_zs, c_zr, c_xs, c_xr, c_ds, c_dr, r_s, r_r,
):
    p = Place(depth)
    half = p.half
    n_exp = EXPERTS

    def load(src, dst, i):
        cp = pltpu.make_async_copy(src, dst, load_sem.at[i])
        cp.start()
        return cp

    loads = [
        load(k_hbm, kg.at[0, p.j], 0), load(v_hbm, vg.at[0, p.j], 1), load(q_hbm, q_in, 2),
        load(res_hbm, res_in, 3), load(gain_hbm, gain_in, 4), load(routes_hbm, routes_in, 5),
        load(gates_hbm, gates_in, 6),
    ]

    barrier = pltpu.get_barrier_semaphore()

    def greet(device):
        pl.semaphore_signal(barrier, inc=1, device_id=device, device_id_type=MESH)

    for device in (p.up, p.down, p.partner, p.sibling):
        greet(device)
    for i in range(1, n_exp):
        greet(p.at(p.z, p.j, lax.rem(p.exp + i, n_exp)))
    home = p.exp // 2
    mine = home == p.j
    for i in range(n_exp):
        f = lax.rem(p.exp + i, n_exp)
        if i == 0:
            @pl.when(jnp.logical_not(mine))
            def _():
                greet(p.at(p.z, home, f))
        else:
            greet(p.at(p.z, home, f))
    for u in range(2):
        for jj in range(PLANE):
            src_e = 2 * p.j + u

            @pl.when(jnp.logical_not(jnp.logical_and(jj == p.j, src_e == p.exp)))
            def _():
                greet(p.at(p.z, jj, src_e))
    pl.semaphore_wait(barrier, 4 + (n_exp - 1) + 16 - 2 * mine.astype(jnp.int32))

    loads[0].wait()
    loads[1].wait()

    def kv_unit(slot, j, u):
        return (vg if u else kg).at[slot, j]

    kv = Gather(p, kv_unit, lambda r, part: r.at[pl.ds(part * (TOK // 2), TOK // 2)], (g_zs, a_zr, g_xs, a_xr, g_ds, a_dr))
    kv.start()

    weight_loads = [load(wg_hbm, wg, 7), load(wu_hbm, wu, 8), load(wd_hbm, wd, 9)]
    for cp in loads[2:]:
        cp.wait()

    for h in range(GROUP):
        qs[pl.ds(h * TOK, TOK), :] = q_in[:, h * HEAD_WIDTH:(h + 1) * HEAD_WIDTH]

    kv.start_partner()

    r_row = [routes_in[k:k + 1, :] for k in range(2)]
    expert_ids = lax.broadcasted_iota(jnp.int32, (EXPERTS, TOK), 0)
    one_hot = [(expert_ids == r_row[k]).astype(F32) for k in range(2)]
    earlier = (
        lax.broadcasted_iota(jnp.int32, (TOK, TOK), 0) < lax.broadcasted_iota(jnp.int32, (TOK, TOK), 1)
    ).astype(BF16)
    before = jnp.dot((one_hot[0] + one_hot[1]).astype(BF16), earlier, preferred_element_type=F32)
    slot_row = [jnp.sum(one_hot[k] * before, axis=0, keepdims=True) for k in range(2)]
    dest = [r_row[k] * PITCH + slot_row[k].astype(jnp.int32) for k in range(2)]
    slot_ids = lax.broadcasted_iota(jnp.int32, (EXPERTS * PITCH, TOK), 0)
    match = [slot_ids == dest[k] for k in range(2)]
    dispatch = jnp.where(jnp.logical_or(match[0], match[1]), 1.0, 0.0).astype(F32)
    mixed[...] = jnp.where(match[0], gates_in[0:1, :], 0.0) + jnp.where(match[1], gates_in[1:2, :], 0.0)

    scale = 1.0 / math.sqrt(HEAD_WIDTH)
    kv_rows = PLANE * TOK

    def attend(slot, first):
        keys = kg[slot].reshape(kv_rows, HEAD_WIDTH)
        vals = vg[slot].reshape(kv_rows, HEAD_WIDTH)
        scores = lax.dot_general(qs[...], keys, (((1,), (1,)), ((), ())), preferred_element_type=F32) * scale
        if first:
            at = lax.broadcasted_iota(jnp.int32, scores.shape, 0)
            for h in range(1, GROUP):
                at = at - jnp.where(lax.broadcasted_iota(jnp.int32, scores.shape, 0) >= h * TOK, TOK, 0)
            seen = lax.broadcasted_iota(jnp.int32, scores.shape, 1) <= at + p.j * TOK
            scores = jnp.where(seen, scores, -1e30)
            top = jnp.max(scores, axis=1, keepdims=True)
            terms = jnp.where(seen, jnp.exp(scores - top), 0.0)
            m_s[...] = top
            l_s[...] = jnp.sum(terms, axis=1, keepdims=True)
            acc_s[...] = jnp.dot(terms.astype(BF16), vals, preferred_element_type=F32)
        else:
            old = m_s[...]
            top = jnp.maximum(old, jnp.max(scores, axis=1, keepdims=True))
            fade = jnp.exp(old - top)
            terms = jnp.exp(scores - top)
            m_s[...] = top
            l_s[...] = l_s[...] * fade + jnp.sum(terms, axis=1, keepdims=True)
            acc_s[...] = acc_s[...] * fade + jnp.dot(terms.astype(BF16), vals, preferred_element_type=F32)

    def attend_all(d):
        for slot in slots_of(d, half):
            if slot == 0:
                attend(0, True)
            else:
                if d == half:
                    seen = p.z >= half
                elif slot % 2 == 1:
                    seen = p.z >= d
                else:
                    seen = p.z + d >= depth

                @pl.when(seen)
                def _(slot=slot):
                    attend(slot, False)

    for d in range(1, half + 1):
        kv.arrive(d)
        kv.arrive_partner(slots_of(d - 1, half))
        kv.arrive_sibling(slots_of(d - 1, half))
        attend_all(d - 1)
    kv.arrive_partner(slots_of(half, half))
    kv.arrive_sibling(slots_of(half, half))
    attend_all(half)

    for h in range(GROUP):
        rows, cols = slice(h * TOK, (h + 1) * TOK), slice(h * HEAD_WIDTH, (h + 1) * HEAD_WIDTH)
        att[:, cols] = (res_in[:, cols].astype(F32) + acc_s[rows, :] / l_s[rows, :]).astype(BF16)
    att_store = pltpu.make_async_copy(att, att_hbm, store_sem.at[0])
    att_store.start()

    stream = att[...].astype(F32)
    squares = lax.dot_general(
        jnp.ones((8, WIDE), F32), stream * stream, (((1,), (1,)), ((), ())),
        precision=lax.Precision.HIGHEST, preferred_element_type=F32,
    )
    ss_buf[p.exp, :, pl.ds(0, TOK)] = squares
    ss_sends = []
    for i in range(1, n_exp):
        other = lax.rem(p.exp + i, n_exp)
        cp = remote(ss_buf.at[p.exp], ss_buf.at[p.exp], ss_s.at[i], ss_r.at[i], p.at(p.z, p.j, other))
        cp.start()
        ss_sends.append(cp)
    rows_out = jnp.dot(dispatch.astype(BF16), att[...], preferred_element_type=F32)
    for i in range(1, n_exp):
        other = lax.rem(p.exp + n_exp - i, n_exp)
        remote(ss_buf.at[other], ss_buf.at[other], ss_s.at[i], ss_r.at[i], p.up).wait_recv()
    total = ss_buf[0, :, pl.ds(0, TOK)]
    for i in range(1, n_exp):
        total = total + ss_buf[i, :, pl.ds(0, TOK)]
    inverse = lax.rsqrt(total / D + 1e-05)
    columns = lax.dot_general(
        dispatch, inverse, (((1,), (1,)), ((), ())), precision=lax.Precision.HIGHEST, preferred_element_type=F32
    )
    normed = (rows_out * columns[:, 0:1] * gain_in[...]).astype(BF16)
    outgoing[...] = normed.reshape(EXPERTS, PITCH, WIDE)

    u_me = lax.rem(p.exp, 2)
    x_sends = []
    for i in range(n_exp):
        f = lax.rem(p.exp + i, n_exp)
        cp = remote(outgoing.at[f], rx.at[u_me, p.j], x_s.at[i], x_r.at[u_me, p.j], p.at(p.z, home, f))
        x_sends.append(cp)
        if i == 0:
            pl.when(jnp.logical_not(mine))(cp.start)

            @pl.when(mine)
            def _():
                rx[u_me, p.j] = outgoing[p.exp]
        else:
            cp.start()

    kv.finish()

    row_ids = lax.broadcasted_iota(jnp.int32, (ROWS, PLANE * PITCH), 0)
    for i in range(1, PLANE):
        row_ids = row_ids + jnp.where(
            lax.broadcasted_iota(jnp.int32, (ROWS, PLANE * PITCH), 0) >= i * CAP, PITCH - CAP, 0
        )
    pack = (row_ids == lax.broadcasted_iota(jnp.int32, (ROWS, PLANE * PITCH), 1)).astype(BF16)

    def columns_of(j, u):
        return pl.ds(pl.multiple_of(j * (2 * WIDE) + u * WIDE, WIDE), WIDE)

    for u in range(2):
        for jj in range(PLANE):
            here = jnp.logical_and(jj == p.j, 2 * p.j + u == p.exp)

            @pl.when(jnp.logical_not(here))
            def _(u=u, jj=jj):
                remote(rx.at[u, jj], rx.at[u, jj], x_s.at[0], x_r.at[u, jj], p.up).wait_recv()

        packed = jnp.dot(pack, rx[u].reshape(PLANE * PITCH, WIDE), preferred_element_type=F32)
        xg[0, :, columns_of(p.j, u)] = packed.astype(BF16)

    def row_unit(slot, j, u):
        return xg.at[slot, :, columns_of(j, u)]

    def row_half(ref, part):
        return ref.at[pl.ds(part * 80, 80 if part == 0 else ROWS - 80)]

    ag = Gather(p, row_unit, row_half, (g_zs, b_zr, g_xs, b_xr, g_ds, b_dr))
    ag.start()
    for cp in weight_loads:
        cp.wait()
    ag.start_partner()

    def hidden(lo, hi):
        count = hi - lo
        rows = xg[lo:hi].reshape(count * ROWS, D)
        gate = jnp.dot(rows, wg[...], preferred_element_type=F32)
        up = jnp.dot(rows, wu[...], preferred_element_type=F32)
        act = gate / (1.0 + jnp.exp(-gate)) * up
        hb[lo:hi] = act.astype(BF16).reshape(count, ROWS, FF_LOCAL)

    def hidden_all(d):
        slots = slots_of(d, half)
        hidden(slots[0], slots[-1] + 1)

    for d in range(1, half + 1):
        ag.arrive(d)
        ag.arrive_partner(slots_of(d - 1, half))
        ag.arrive_sibling(slots_of(d - 1, half))
        hidden_all(d - 1)
    ag.arrive_partner(slots_of(half, half))
    ag.arrive_sibling(slots_of(half, half))
    hidden_all(half)

    sent = []

    def send(src, dst, ss, rs, device):
        cp = remote(src, dst, ss, rs, device)
        cp.start()
        sent.append(cp)

    def wait_for(ref, rs):
        remote(ref, ref, c_zs.at[0, 0], rs, p.up).wait_recv()

    def wide_columns(j):
        return pl.ds(pl.multiple_of(j * (2 * WIDE), 2 * WIDE), 2 * WIDE)

    def produce(slot):
        def part(n, _):
            cols = pl.ds(pl.multiple_of(n * WIDE, WIDE), WIDE)
            yb[slot, :, cols] = jnp.dot(hb[slot], wd[:, cols], preferred_element_type=F32).astype(BF16)
            return 0

        lax.fori_loop(0, D // WIDE, part, 0)
        for k, j in enumerate((p.jc, p.jcp)):
            send(yb.at[slot, :, wide_columns(j)], dr_buf.at[slot, k], c_ds.at[slot, k], c_dr.at[slot, k], p.sibling)

    def for_partner(slot):
        for k in range(2):
            wait_for(dr_buf.at[slot, k], c_dr.at[slot, k])
        cols = columns_of(p.jp, 1)
        yb[slot, :, cols] = (yb[slot, :, cols].astype(F32) + dr_buf[slot, 1, :, WIDE:].astype(F32)).astype(BF16)
        send(yb.at[slot, :, cols], xr_buf.at[slot], c_xs.at[slot], c_xr.at[slot], p.partner)

    def halves(ref, part):
        return ref.at[:, pl.ds(part * (WIDE // 2), WIDE // 2)]

    def reduce_slot(slot, d):
        for k, j, u in ((0, p.j, 0), (2, p.jp, 0), (1, p.j, 1)):
            cols = columns_of(j, u)
            own = k != 2
            total = yb[slot, :, cols].astype(F32)
            total = total + dr_buf[slot, 0 if own else 1, :, pl.ds(u * WIDE, WIDE)].astype(F32)
            if k == 1:
                wait_for(xr_buf.at[slot], c_xr.at[slot])
                total = total + xr_buf[slot].astype(F32)
            if d == half:
                yb[slot, :, cols] = total.astype(BF16)
            elif d == half - 1:
                part = 0 if slot % 2 == 1 else 1
                wait_for(halves(zr_buf.at[slot, k], part), c_zr.at[slot, k])
                cut = slice(part * (WIDE // 2), (part + 1) * (WIDE // 2))
                keep = slice((1 - part) * (WIDE // 2), (2 - part) * (WIDE // 2))
                zr = zr_buf[slot, k, :, cut].astype(F32)
                base = j * (2 * WIDE) + u * WIDE
                for piece, value in ((cut, total[:, cut] + zr), (keep, total[:, keep])):
                    at = pl.ds(pl.multiple_of(base + piece.start, WIDE // 2), WIDE // 2)
                    yb[slot, :, at] = value.astype(BF16)
            else:
                sources = (0, 2 * half - 1) if slot == 0 else (slot,)
                for i in sources:
                    wait_for(zr_buf.at[i, k], c_zr.at[i, k])
                    total = total + zr_buf[i, k].astype(F32)
                yb[slot, :, cols] = total.astype(BF16)
            if d == 0:
                if k == 2:
                    send(yb.at[slot, :, cols], xr_buf.at[8], c_xs.at[8], c_xr.at[8], p.partner)
            elif d == half:
                for part in (0, 1):
                    to = 2 * (d - 1) - 1 + part
                    base = j * (2 * WIDE) + u * WIDE + part * (WIDE // 2)
                    send(
                        yb.at[slot, :, pl.ds(pl.multiple_of(base, WIDE // 2), WIDE // 2)],
                        halves(zr_buf.at[to, k], part),
                        c_zs.at[slot + part, k], c_zr.at[to, k], p.down if part == 0 else p.up,
                    )
            else:
                plus = slot % 2 == 1
                if d == 1:
                    to = 0 if plus else 2 * half - 1
                else:
                    to = slot - 2
                send(
                    yb.at[slot, :, cols], zr_buf.at[to, k], c_zs.at[slot, k], c_zr.at[to, k],
                    p.down if plus else p.up,
                )

    order = [(d, s) for d in range(half, -1, -1) for s in slots_of(d, half)]
    produce(order[0][1])
    for d in range(half, -1, -1):
        ahead = slots_of(d - 1, half) if d > 0 else ()
        for s in slots_of(d, half):
            for_partner(s)
        for s in ahead:
            produce(s)
        for s in slots_of(d, half):
            reduce_slot(s, d)

    wait_for(xr_buf.at[8], c_xr.at[8])
    first = columns_of(p.j, 0)
    fb[0] = (yb[0, :, first].astype(F32) + xr_buf[8].astype(F32)).astype(BF16)
    fb[1] = yb[0, :, columns_of(p.j, 1)]

    for u in range(2):
        spread = lax.dot_general(pack, fb[u], (((0,), (0,)), ((), ())), preferred_element_type=F32)
        rb[u] = spread.astype(BF16).reshape(PLANE, PITCH, WIDE)
    r_sends = []
    for u in range(2):
        for jj in range(PLANE):
            here = jnp.logical_and(jj == p.j, 2 * p.j + u == p.exp)
            cp = remote(rb.at[u, jj], ret.at[p.exp], r_s.at[u * PLANE + jj], r_r.at[p.exp], p.at(p.z, jj, 2 * p.j + u))
            r_sends.append((here, cp))
            pl.when(jnp.logical_not(here))(cp.start)

            @pl.when(here)
            def _(u=u, jj=jj):
                ret[p.exp] = rb[u, jj]

    ag.finish()
    for cp in sent:
        cp.wait_send()
    for cp in ss_sends:
        cp.wait_send()
    for i, cp in enumerate(x_sends):
        if i == 0:
            pl.when(jnp.logical_not(mine))(cp.wait_send)
        else:
            cp.wait_send()

    for i in range(n_exp):
        f = lax.rem(p.exp + i, n_exp)
        cp = remote(ret.at[f], ret.at[f], r_s.at[0], r_r.at[f], p.up)
        if i == 0:
            pl.when(jnp.logical_not(mine))(cp.wait_recv)
        else:
            cp.wait_recv()
    returned = ret[...].reshape(EXPERTS * PITCH, WIDE).astype(F32)
    mix = lax.dot_general(
        mixed[...], returned, (((0,), (0,)), ((), ())), precision=lax.Precision.HIGHEST, preferred_element_type=F32
    )
    out_v[...] = (att[...].astype(F32) + mix).astype(BF16)
    out_store = pltpu.make_async_copy(out_v, out_hbm, store_sem.at[1])
    out_store.start()
    for here, cp in r_sends:
        pl.when(jnp.logical_not(here))(cp.wait_send)
    att_store.wait()
    out_store.wait()


def shards(depth, queries, keys, values, residual, norm_gain, routes, gates, w_gate, w_up, w_down):
    any_spec = pl.BlockSpec(memory_space=pl.ANY)
    slots = depth
    vmem, dma = pltpu.VMEM, pltpu.SemaphoreType.DMA
    tok_block = jax.ShapeDtypeStruct((TOK, WIDE), BF16)
    scratch = [
        vmem((TOK, WIDE), BF16), vmem((TOK, WIDE), BF16), vmem((1, WIDE), F32), vmem((2, TOK), jnp.int32),
        vmem((2, TOK), F32), vmem((D, FF_LOCAL), BF16), vmem((D, FF_LOCAL), BF16), vmem((FF_LOCAL, D), BF16),
        vmem((slots, PLANE, TOK, HEAD_WIDTH), BF16), vmem((slots, PLANE, TOK, HEAD_WIDTH), BF16),
        vmem((GROUP * TOK, HEAD_WIDTH), BF16), vmem((GROUP * TOK, 1), F32), vmem((GROUP * TOK, 1), F32),
        vmem((GROUP * TOK, HEAD_WIDTH), F32), vmem((TOK, WIDE), BF16), vmem((EXPERTS, 8, 128), F32),
        vmem((EXPERTS, PITCH, WIDE), BF16), vmem((2, PLANE, PITCH, WIDE), BF16),
        vmem((slots, ROWS, D), BF16), vmem((slots, ROWS, FF_LOCAL), BF16), vmem((slots, ROWS, D), BF16),
        vmem((slots, 2, ROWS, 2 * WIDE), BF16), vmem((slots, 3, ROWS, WIDE), BF16), vmem((9, ROWS, WIDE), BF16),
        vmem((2, ROWS, WIDE), BF16), vmem((2, PLANE, PITCH, WIDE), BF16), vmem((EXPERTS, PITCH, WIDE), BF16),
        vmem((EXPERTS * PITCH, TOK), F32), vmem((TOK, WIDE), BF16),
        dma((10,)), dma((2,)),
        dma((9, 3)), dma((9,)), dma((8, 4)),
        dma((9, 3)), dma((9,)), dma((8, 4)),
        dma((9, 3)), dma((9,)), dma((8, 4)),
        dma((8,)), dma((8,)), dma((8,)), dma((2, PLANE)),
        dma((9, 3)), dma((9, 3)), dma((9,)), dma((9,)), dma((8, 2)), dma((8, 2)),
        dma((8,)), dma((8,)),
    ]
    return pl.pallas_call(
        functools.partial(kernel, depth),
        out_shape=(tok_block, tok_block),
        in_specs=[any_spec] * 10,
        out_specs=(any_spec, any_spec),
        scratch_shapes=scratch,
        compiler_params=pltpu.CompilerParams(
            collective_id=0, has_side_effects=True, vmem_limit_bytes=64 * 1024 * 1024 - 65536
        ),
    )(
        queries, keys, values, residual, norm_gain.reshape(1, WIDE), routes.T, gates.T,
        w_gate[0], w_up[0], w_down[0],
    )


def solution(mesh):
    in_specs = (
        P("seq", "exp"), P("seq", "exp"), P("seq", "exp"), P("seq", "exp"), P("exp"), P("seq", None), P("seq", None),
        P("exp", None, "seq"), P("exp", None, "seq"), P("exp", "seq", None),
    )
    body = functools.partial(shards, mesh.shape["seq"] // PLANE)
    return jax.shard_map(body, mesh=mesh, in_specs=in_specs, out_specs=(P("seq", "exp"), P("seq", "exp")), check_vma=False)
```

time: 432 us -> 167 us (0.39); the launches traced: 427 us -> 166 us
  waiting for transfers between devices: 200 us -> 0 us
  Pallas kernels: 0 us -> 150 us
  blocking collectives: 126 us -> 0 us
  matrix products: 31.4 us -> 0 us
  starting transfers between devices: 30.5 us -> 0 us
  between operations: 14.9 us -> 0.64 us
  other arithmetic: 4.52 us -> 0 us
    all_gather x2 -> x0, waiting for transfers between devices: 185 us -> none  [the longest x1 106 us: shards(): flat_rows = lax.all_gather(local_rows, 'seq', axis=0, tiled=True)]
    pallas_call x0 -> x1, Pallas kernels: none -> 150 us  [shards(): pl.pallas_call(functools.partial(kernel, depth), out_shape=(tok_block, to...]
    unnamed x1 -> x0, blocking collectives: 117 us -> none
    dot_general x6 -> x0, matrix products: 31.4 us -> none  [the longest x1 17.4 us: shards(): jnp.dot(hidden, down_mat, preferred_element_type=jnp.float32)]
    unnamed x4 -> x0, starting transfers between devices: 20 us -> none
    all_to_all x2 -> x0, starting transfers between devices: 10.5 us -> none  [the longest x1 5.76 us: sent_to_all(): lax.all_to_all(jnp.broadcast_to(value[None], (peers, *value.shape)), axis...]
    all_to_all x2 -> x0, waiting for transfers between devices: 9.68 us -> none  [the longest x1 5.95 us: shards(): lax.all_to_all(expert_out, 'exp', split_axis=2, concat_axis=0, tiled=True)]
    all_to_all x1 -> x0, blocking collectives: 9.13 us -> none  [shards(): lax.all_to_all(outgoing, 'exp', split_axis=0, concat_axis=2, tiled=True)]
  transfers between devices with their start and end apart: 8 -> 0, of which waited for: 5 -> 0; matrix products, arithmetic and copies ran while one was open for 1% -> 0% of each run, Pallas kernels for 0% -> 0%
where the time goes in v1:
time: 167 us; the launch traced here: 166 us
  Pallas kernels  150 us (90%)
  local copies, waits for them, and re-layouts  16 us (10%)
    pallas_call x1, Pallas kernels, shards(): pl.pallas_call(functools.partial(kernel, depth), out_shape=(tok_block, to...  150 us
    unnamed x4, local copies, waits for them, and re-layouts  16 us

profile of v1, /device:TPU:13, one launch (start us, length us, event | category | flops | bytes accessed | tf_op | source)
XLA Modules:
  0.0 166.4 jit_solution(14025867827140742509)
XLA Ops:
  0.6 6.4 %copy.12 = bf16[1,4096,448]{2,1,0:T(8,128)(2,1)} copy(bf16[1,4096,448]{1,2,0:T(8,128)(2,1)} %param.17) | data formatting | bytes 7340032 | tf_op args[7]
  7.0 6.5 %copy.13 = bf16[1,4096,448]{2,1,0:T(8,128)(2,1)} copy(bf16[1,4096,448]{1,2,0:T(8,128)(2,1)} %param.18) | data formatting | bytes 7340032 | tf_op args[8]
  13.5 149.7 %shard_map.113 = (bf16[96,512]{1,0:T(8,128)(2,1)}, bf16[96,512]{1,0:T(8,128)(2,1)}) custom-call(bf16[96,512]{1,0:T(8,128)(2,1)} %q_hbm.1, bf16[96,128]{1,0:T(8,128)(2,1)} %k_hbm.1, bf16[96,128]{1,0:T(8,128)(2,1)} %v_hbm.1, bf16[96,512]{1,0:T(8,128)(2,1)} %res_hbm.1, f32[1,512]{1,0:T(1,128)} %bitcast.9, s32[2,96]{1,0:T(2,128)} %bitcast.10, f32[2,96]{1,0:T(2,128)} %bitcast.11, ...), custom_call_target="tpu_custom_call" | custom-call | tf_op jit(solution)/shard_map/pallas_call | solution.py:550
  163.3 1.5 copy.16
  164.8 1.5 copy.17

commit v2 on v1

--- a/solution.py
+++ b/solution.py
@@ -20,6 +20,7 @@
 WIDE = 512
 FF_LOCAL = 448
 MESH = pl.DeviceIdType.MESH
+VMEM_BYTES = 63 * 1024 * 1024
 F32 = jnp.float32
 BF16 = jnp.bfloat16
 
@@ -38,6 +39,8 @@
         self.jcp = (1 - xh) * 2 + (1 - c)
         self.up = self.at(lax.rem(self.z + 1, depth), self.j)
         self.down = self.at(lax.rem(self.z + depth - 1, depth), self.j)
+        self.up_other = self.at(lax.rem(self.z + 1, depth), self.jp)
+        self.down_other = self.at(lax.rem(self.z + depth - 1, depth), self.jp)
         self.partner = self.at(self.z, self.jp)
         self.sibling = self.at(self.z, self.jc)
 
@@ -80,15 +83,15 @@
     def across(self, slot, k, j, u):
         self.send(self.unit(slot, j, u), self.ds.at[slot, k], self.dr.at[slot, k], self.p.sibling)
 
-    def start(self):
+    def start(self, u):
         p = self.p
-        self.send(self.unit(0, p.j, 0), self.xs.at[8], self.xr.at[8], p.partner)
-        for u in (1, 0):
-            self.ring(0, True, 0, u, p.j, u)
-            self.ring(0, False, 0, u, p.j, u)
-        self.send(self.unit(0, p.j, 1), self.xs.at[0], self.xr.at[0], p.partner)
-        self.across(0, 0, p.j, 0)
-        self.across(0, 1, p.j, 1)
+        if u == 0:
+            self.send(self.unit(0, p.j, 0), self.xs.at[8], self.xr.at[8], p.partner)
+        self.ring(0, True, 0, u, p.j, u)
+        self.ring(0, False, 0, u, p.j, u)
+        self.across(0, u, p.j, u)
+        if u == 0:
+            self.send(self.unit(0, p.j, 1), self.xs.at[0], self.xr.at[0], p.partner)
 
     def start_partner(self):
         p = self.p
@@ -97,7 +100,7 @@
         self.ring(0, False, 0, 2, p.jp, 0)
         self.across(0, 2, p.jp, 0)
 
-    def arrive(self, d):
+    def arrive(self, d, after):
         p, h = self.p, self.p.half
         for k, own, u in ((1, True, 1), (0, True, 0), (2, False, 0)):
             j = p.j if own else p.jp
@@ -116,6 +119,7 @@
                 if k == 1:
                     self.send(self.unit(slot, j, 1), self.xs.at[slot], self.xr.at[slot], p.partner)
                 self.across(slot, k, j, u)
+            after(k)
 
     def arrive_partner(self, slots):
         for slot in slots:
@@ -133,6 +137,78 @@
             cp.wait_send()
 
 
+class KvGather:
+    def __init__(self, place, kv, sems):
+        self.p, self.kv = place, kv
+        self.zs, self.zr, self.xs, self.xr, self.ds, self.dr = sems
+        self.sent = []
+
+    def send(self, ref, ss, rs, device):
+        cp = remote(ref, ref, ss, rs, device)
+        cp.start()
+        self.sent.append(cp)
+
+    def got(self, ref, rs):
+        remote(ref, ref, self.zs.at[0, 0], rs, self.p.up).wait_recv()
+
+    def ring(self, src_slot, plus, d, k):
+        p, h = self.p, self.p.half
+        sem = 2 * (d + 1) - 1 if plus else 2 * (d + 1)
+        src, dst = self.kv.at[src_slot, p.j], self.kv.at[min(sem, 2 * h - 1), p.j]
+        if d + 1 == h:
+            part = 0 if plus else 1
+            src, dst = src.at[part], dst.at[part]
+        device = ((p.up, p.up_other) if plus else (p.down, p.down_other))[k]
+        cp = remote(src, dst, self.zs.at[sem, k], self.zr.at[sem, k], device)
+        cp.start()
+        self.sent.append(cp)
+
+    def across(self, slot, k, j):
+        self.send(self.kv.at[slot, j], self.ds.at[slot, k], self.dr.at[slot, k], self.p.sibling)
+
+    def start(self):
+        p = self.p
+        for k in (0, 1):
+            self.ring(0, True, 0, k)
+            self.ring(0, False, 0, k)
+        self.send(self.kv.at[0, p.j], self.xs.at[0], self.xr.at[0], p.partner)
+        self.across(0, 0, p.j)
+
+    def arrive(self, d):
+        p, h = self.p, self.p.half
+        for slot in slots_of(d, h):
+            if d < h:
+                self.got(self.kv.at[slot, p.j], self.zr.at[slot, 0])
+                for k in (0, 1):
+                    self.ring(slot, slot % 2 == 1, d, k)
+            else:
+                for part in (0, 1):
+                    self.got(self.kv.at[slot, p.j, part], self.zr.at[slot + part, 0])
+            self.across(slot, 0, p.j)
+
+    def arrive_other(self, d):
+        p, h = self.p, self.p.half
+        for slot in slots_of(d, h):
+            if d == 0:
+                self.got(self.kv.at[slot, p.jp], self.xr.at[0])
+            elif d < h:
+                self.got(self.kv.at[slot, p.jp], self.zr.at[slot, 1])
+            else:
+                for part in (0, 1):
+                    self.got(self.kv.at[slot, p.jp, part], self.zr.at[slot + part, 1])
+            self.across(slot, 1, p.jp)
+
+    def arrive_sibling(self, slots):
+        p = self.p
+        for slot in slots:
+            for k, j in enumerate((p.jc, p.jcp)):
+                self.got(self.kv.at[slot, j], self.dr.at[slot, k])
+
+    def finish(self):
+        for cp in self.sent:
+            cp.wait_send()
+
+
 def slots_of(d, half):
     if d == 0:
         return (0,)
@@ -142,10 +218,10 @@
 def kernel(
     depth,
     q_hbm, k_hbm, v_hbm, res_hbm, gain_hbm, routes_hbm, gates_hbm, wg_hbm, wu_hbm, wd_hbm,
-    att_hbm, out_hbm,
+    attn_out, mix_out,
     q_in, res_in, gain_in, routes_in, gates_in, wg, wu, wd,
-    kg, vg, qs, m_s, l_s, acc_s, att, ss_buf, outgoing, rx, xg, hb, yb, dr_buf, zr_buf, xr_buf, fb, rb, ret, mixed, out_v,
-    load_sem, store_sem, g_zs, g_xs, g_ds, a_zr, a_xr, a_dr, b_zr, b_xr, b_dr,
+    kvg, qs, m_s, l_s, acc_s, att, ss_buf, outgoing, rx, xg, hb, yb, dr_buf, zr_buf, xr_buf, fb, rb, ret, mixed,
+    load_sem, g_zs, g_xs, g_ds, a_zr, a_xr, a_dr, b_zr, b_xr, b_dr,
     ss_s, ss_r, x_s, x_r, c_zs, c_zr, c_xs, c_xr, c_ds, c_dr, r_s, r_r,
 ):
     p = Place(depth)
@@ -158,7 +234,7 @@
         return cp
 
     loads = [
-        load(k_hbm, kg.at[0, p.j], 0), load(v_hbm, vg.at[0, p.j], 1), load(q_hbm, q_in, 2),
+        load(k_hbm, kvg.at[0, p.j, 0], 0), load(v_hbm, kvg.at[0, p.j, 1], 1), load(q_hbm, q_in, 2),
         load(res_hbm, res_in, 3), load(gain_hbm, gain_in, 4), load(routes_hbm, routes_in, 5),
         load(gates_hbm, gates_in, 6),
     ]
@@ -168,7 +244,7 @@
     def greet(device):
         pl.semaphore_signal(barrier, inc=1, device_id=device, device_id_type=MESH)
 
-    for device in (p.up, p.down, p.partner, p.sibling):
+    for device in (p.up, p.down, p.up_other, p.down_other, p.partner, p.sibling):
         greet(device)
     for i in range(1, n_exp):
         greet(p.at(p.z, p.j, lax.rem(p.exp + i, n_exp)))
@@ -189,15 +265,12 @@
             @pl.when(jnp.logical_not(jnp.logical_and(jj == p.j, src_e == p.exp)))
             def _():
                 greet(p.at(p.z, jj, src_e))
-    pl.semaphore_wait(barrier, 4 + (n_exp - 1) + 16 - 2 * mine.astype(jnp.int32))
+    pl.semaphore_wait(barrier, 6 + (n_exp - 1) + 16 - 2 * mine.astype(jnp.int32))
 
     loads[0].wait()
     loads[1].wait()
 
-    def kv_unit(slot, j, u):
-        return (vg if u else kg).at[slot, j]
-
-    kv = Gather(p, kv_unit, lambda r, part: r.at[pl.ds(part * (TOK // 2), TOK // 2)], (g_zs, a_zr, g_xs, a_xr, g_ds, a_dr))
+    kv = KvGather(p, kvg, (g_zs, a_zr, g_xs, a_xr, g_ds, a_dr))
     kv.start()
 
     weight_loads = [load(wg_hbm, wg, 7), load(wu_hbm, wu, 8), load(wd_hbm, wd, 9)]
@@ -206,8 +279,6 @@
 
     for h in range(GROUP):
         qs[pl.ds(h * TOK, TOK), :] = q_in[:, h * HEAD_WIDTH:(h + 1) * HEAD_WIDTH]
-
-    kv.start_partner()
 
     r_row = [routes_in[k:k + 1, :] for k in range(2)]
     expert_ids = lax.broadcasted_iota(jnp.int32, (EXPERTS, TOK), 0)
@@ -227,8 +298,8 @@
     kv_rows = PLANE * TOK
 
     def attend(slot, first):
-        keys = kg[slot].reshape(kv_rows, HEAD_WIDTH)
-        vals = vg[slot].reshape(kv_rows, HEAD_WIDTH)
+        keys = kvg[slot, :, 0].reshape(kv_rows, HEAD_WIDTH)
+        vals = kvg[slot, :, 1].reshape(kv_rows, HEAD_WIDTH)
         scores = lax.dot_general(qs[...], keys, (((1,), (1,)), ((), ())), preferred_element_type=F32) * scale
         if first:
             at = lax.broadcasted_iota(jnp.int32, scores.shape, 0)
@@ -268,18 +339,18 @@
 
     for d in range(1, half + 1):
         kv.arrive(d)
-        kv.arrive_partner(slots_of(d - 1, half))
+        kv.arrive_other(d - 1)
         kv.arrive_sibling(slots_of(d - 1, half))
         attend_all(d - 1)
-    kv.arrive_partner(slots_of(half, half))
+    kv.arrive_other(half)
     kv.arrive_sibling(slots_of(half, half))
     attend_all(half)
 
     for h in range(GROUP):
         rows, cols = slice(h * TOK, (h + 1) * TOK), slice(h * HEAD_WIDTH, (h + 1) * HEAD_WIDTH)
-        att[:, cols] = (res_in[:, cols].astype(F32) + acc_s[rows, :] / l_s[rows, :]).astype(BF16)
-    att_store = pltpu.make_async_copy(att, att_hbm, store_sem.at[0])
-    att_store.start()
+        attn = acc_s[rows, :] / l_s[rows, :]
+        attn_out[:, cols] = attn
+        att[:, cols] = (res_in[:, cols].astype(F32) + attn).astype(BF16)
 
     stream = att[...].astype(F32)
     squares = lax.dot_general(
@@ -334,7 +405,14 @@
     def columns_of(j, u):
         return pl.ds(pl.multiple_of(j * (2 * WIDE) + u * WIDE, WIDE), WIDE)
 
-    for u in range(2):
+    def row_unit(slot, j, u):
+        return xg.at[slot, :, columns_of(j, u)]
+
+    def row_half(ref, part):
+        return ref.at[pl.ds(part * 80, 80 if part == 0 else ROWS - 80)]
+
+    ag = Gather(p, row_unit, row_half, (g_zs, b_zr, g_xs, b_xr, g_ds, b_dr))
+    for u in (1, 0):
         for jj in range(PLANE):
             here = jnp.logical_and(jj == p.j, 2 * p.j + u == p.exp)
 
@@ -344,15 +422,7 @@
 
         packed = jnp.dot(pack, rx[u].reshape(PLANE * PITCH, WIDE), preferred_element_type=F32)
         xg[0, :, columns_of(p.j, u)] = packed.astype(BF16)
-
-    def row_unit(slot, j, u):
-        return xg.at[slot, :, columns_of(j, u)]
-
-    def row_half(ref, part):
-        return ref.at[pl.ds(part * 80, 80 if part == 0 else ROWS - 80)]
-
-    ag = Gather(p, row_unit, row_half, (g_zs, b_zr, g_xs, b_xr, g_ds, b_dr))
-    ag.start()
+        ag.start(u)
     for cp in weight_loads:
         cp.wait()
     ag.start_partner()
@@ -360,23 +430,14 @@
     def hidden(lo, hi):
         count = hi - lo
         rows = xg[lo:hi].reshape(count * ROWS, D)
-        gate = jnp.dot(rows, wg[...], preferred_element_type=F32)
-        up = jnp.dot(rows, wu[...], preferred_element_type=F32)
+        gate = lax.dot_general(rows, wg[...], (((1,), (1,)), ((), ())), preferred_element_type=F32)
+        up = lax.dot_general(rows, wu[...], (((1,), (1,)), ((), ())), preferred_element_type=F32)
         act = gate / (1.0 + jnp.exp(-gate)) * up
         hb[lo:hi] = act.astype(BF16).reshape(count, ROWS, FF_LOCAL)
 
     def hidden_all(d):
         slots = slots_of(d, half)
         hidden(slots[0], slots[-1] + 1)
-
-    for d in range(1, half + 1):
-        ag.arrive(d)
-        ag.arrive_partner(slots_of(d - 1, half))
-        ag.arrive_sibling(slots_of(d - 1, half))
-        hidden_all(d - 1)
-    ag.arrive_partner(slots_of(half, half))
-    ag.arrive_sibling(slots_of(half, half))
-    hidden_all(half)
 
     sent = []
 
@@ -411,8 +472,8 @@
     def halves(ref, part):
         return ref.at[:, pl.ds(part * (WIDE // 2), WIDE // 2)]
 
-    def reduce_slot(slot, d):
-        for k, j, u in ((0, p.j, 0), (2, p.jp, 0), (1, p.j, 1)):
+    def reduce_unit(slot, d, k):
+        for j, u in (((p.j, 0), (p.j, 1), (p.jp, 0))[k],):
             cols = columns_of(j, u)
             own = k != 2
             total = yb[slot, :, cols].astype(F32)
@@ -461,27 +522,49 @@
                     p.down if plus else p.up,
                 )
 
-    order = [(d, s) for d in range(half, -1, -1) for s in slots_of(d, half)]
-    produce(order[0][1])
-    for d in range(half, -1, -1):
-        ahead = slots_of(d - 1, half) if d > 0 else ()
-        for s in slots_of(d, half):
-            for_partner(s)
-        for s in ahead:
-            produce(s)
-        for s in slots_of(d, half):
-            reduce_slot(s, d)
-
-    wait_for(xr_buf.at[8], c_xr.at[8])
-    first = columns_of(p.j, 0)
-    fb[0] = (yb[0, :, first].astype(F32) + xr_buf[8].astype(F32)).astype(BF16)
-    fb[1] = yb[0, :, columns_of(p.j, 1)]
-
-    for u in range(2):
+    last, next_in = slots_of(half, half), slots_of(half - 1, half)
+    for d in range(1, half + 1):
+        near = slots_of(d - 1, half)
+
+        def between(k):
+            if k == 1:
+                ag.arrive_partner(near)
+            elif k == 0:
+                ag.arrive_sibling(near)
+                hidden_all(d - 1)
+
+        ag.arrive(d, between)
+    ag.arrive_partner(last)
+    produce(next_in[0])
+    ag.arrive_sibling(last)
+
+    hidden_all(half)
+    for s in last:
+        produce(s)
+    for_partner(next_in[0])
+    for s in next_in[1:]:
+        produce(s)
+    for s in last:
+        for_partner(s)
+    for d in range(half, 0, -1):
+        for k in (0, 2):
+            for s in slots_of(d, half):
+                reduce_unit(s, d, k)
+        for s in slots_of(d - 1, half):
+            if s != next_in[0]:
+                for_partner(s)
+        if d < half:
+            for s in slots_of(d + 1, half):
+                reduce_unit(s, d + 1, 1)
+        if d > 1:
+            for s in slots_of(d - 2, half):
+                produce(s)
+
+    r_sends = []
+
+    def give_back(u):
         spread = lax.dot_general(pack, fb[u], (((0,), (0,)), ((), ())), preferred_element_type=F32)
         rb[u] = spread.astype(BF16).reshape(PLANE, PITCH, WIDE)
-    r_sends = []
-    for u in range(2):
         for jj in range(PLANE):
             here = jnp.logical_and(jj == p.j, 2 * p.j + u == p.exp)
             cp = remote(rb.at[u, jj], ret.at[p.exp], r_s.at[u * PLANE + jj], r_r.at[p.exp], p.at(p.z, jj, 2 * p.j + u))
@@ -489,8 +572,19 @@
             pl.when(jnp.logical_not(here))(cp.start)
 
             @pl.when(here)
-            def _(u=u, jj=jj):
+            def _():
                 ret[p.exp] = rb[u, jj]
+
+    reduce_unit(0, 0, 2)
+    reduce_unit(0, 0, 0)
+    for s in slots_of(1, half):
+        reduce_unit(s, 1, 1)
+    wait_for(xr_buf.at[8], c_xr.at[8])
+    fb[0] = (yb[0, :, columns_of(p.j, 0)].astype(F32) + xr_buf[8].astype(F32)).astype(BF16)
+    give_back(0)
+    reduce_unit(0, 0, 1)
+    fb[1] = yb[0, :, columns_of(p.j, 1)]
+    give_back(1)
 
     ag.finish()
     for cp in sent:
@@ -511,55 +605,53 @@
         else:
             cp.wait_recv()
     returned = ret[...].reshape(EXPERTS * PITCH, WIDE).astype(F32)
-    mix = lax.dot_general(
+    mix_out[...] = lax.dot_general(
         mixed[...], returned, (((0,), (0,)), ((), ())), precision=lax.Precision.HIGHEST, preferred_element_type=F32
     )
-    out_v[...] = (att[...].astype(F32) + mix).astype(BF16)
-    out_store = pltpu.make_async_copy(out_v, out_hbm, store_sem.at[1])
-    out_store.start()
     for here, cp in r_sends:
         pl.when(jnp.logical_not(here))(cp.wait_send)
-    att_store.wait()
-    out_store.wait()
 
 
 def shards(depth, queries, keys, values, residual, norm_gain, routes, gates, w_gate, w_up, w_down):
-    any_spec = pl.BlockSpec(memory_space=pl.ANY)
+    hbm_spec = pl.BlockSpec(memory_space=pltpu.HBM)
+    vmem_spec = pl.BlockSpec(memory_space=pltpu.VMEM)
     slots = depth
     vmem, dma = pltpu.VMEM, pltpu.SemaphoreType.DMA
-    tok_block = jax.ShapeDtypeStruct((TOK, WIDE), BF16)
+    tok_block = jax.ShapeDtypeStruct((TOK, WIDE), F32)
     scratch = [
         vmem((TOK, WIDE), BF16), vmem((TOK, WIDE), BF16), vmem((1, WIDE), F32), vmem((2, TOK), jnp.int32),
-        vmem((2, TOK), F32), vmem((D, FF_LOCAL), BF16), vmem((D, FF_LOCAL), BF16), vmem((FF_LOCAL, D), BF16),
-        vmem((slots, PLANE, TOK, HEAD_WIDTH), BF16), vmem((slots, PLANE, TOK, HEAD_WIDTH), BF16),
+        vmem((2, TOK), F32), vmem((FF_LOCAL, D), BF16), vmem((FF_LOCAL, D), BF16), vmem((FF_LOCAL, D), BF16),
+        vmem((slots, PLANE, 2, TOK, HEAD_WIDTH), BF16),
         vmem((GROUP * TOK, HEAD_WIDTH), BF16), vmem((GROUP * TOK, 1), F32), vmem((GROUP * TOK, 1), F32),
         vmem((GROUP * TOK, HEAD_WIDTH), F32), vmem((TOK, WIDE), BF16), vmem((EXPERTS, 8, 128), F32),
         vmem((EXPERTS, PITCH, WIDE), BF16), vmem((2, PLANE, PITCH, WIDE), BF16),
         vmem((slots, ROWS, D), BF16), vmem((slots, ROWS, FF_LOCAL), BF16), vmem((slots, ROWS, D), BF16),
         vmem((slots, 2, ROWS, 2 * WIDE), BF16), vmem((slots, 3, ROWS, WIDE), BF16), vmem((9, ROWS, WIDE), BF16),
         vmem((2, ROWS, WIDE), BF16), vmem((2, PLANE, PITCH, WIDE), BF16), vmem((EXPERTS, PITCH, WIDE), BF16),
-        vmem((EXPERTS * PITCH, TOK), F32), vmem((TOK, WIDE), BF16),
-        dma((10,)), dma((2,)),
+        vmem((EXPERTS * PITCH, TOK), F32),
+        dma((10,)),
         dma((9, 3)), dma((9,)), dma((8, 4)),
-        dma((9, 3)), dma((9,)), dma((8, 4)),
+        dma((9, 2)), dma((1,)), dma((8, 2)),
         dma((9, 3)), dma((9,)), dma((8, 4)),
         dma((8,)), dma((8,)), dma((8,)), dma((2, PLANE)),
         dma((9, 3)), dma((9, 3)), dma((9,)), dma((9,)), dma((8, 2)), dma((8, 2)),
         dma((8,)), dma((8,)),
     ]
-    return pl.pallas_call(
+    attn, mix = pl.pallas_call(
         functools.partial(kernel, depth),
         out_shape=(tok_block, tok_block),
-        in_specs=[any_spec] * 10,
-        out_specs=(any_spec, any_spec),
+        in_specs=[hbm_spec] * 10,
+        out_specs=(vmem_spec, vmem_spec),
         scratch_shapes=scratch,
         compiler_params=pltpu.CompilerParams(
-            collective_id=0, has_side_effects=True, vmem_limit_bytes=64 * 1024 * 1024 - 65536
+            collective_id=0, has_side_effects=True, vmem_limit_bytes=VMEM_BYTES
         ),
     )(
         queries, keys, values, residual, norm_gain.reshape(1, WIDE), routes.T, gates.T,
-        w_gate[0], w_up[0], w_down[0],
+        w_gate[0].T, w_up[0].T, w_down[0],
     )
+    attended = lax.reduce_precision(residual.astype(F32) + attn, 8, 7)
+    return attended.astype(BF16), (attended + mix).astype(BF16)
 
 
 def solution(mesh):

time: 167 us -> 141 us (0.84)
  local copies, waits for them, and re-layouts: 16 us -> 0.01 us
  Pallas kernels: 150 us -> 139 us
  other arithmetic: 0 us -> 1.74 us
    unnamed x4 -> x2, local copies, waits for them, and re-layouts: 16 us -> 0.01 us
    pallas_call x1, Pallas kernels: 150 us -> 139 us  [shards(): pl.pallas_call(functools.partial(kernel, depth), out_shape=(tok_block, to...]
    convert_element_type x0 -> x1, other arithmetic: none -> 1.74 us  [shards(): return (attended.astype(BF16), (attended + mix).astype(BF16))]
where the time goes in v2:
time: 141 us
  Pallas kernels  139 us (99%)
  other arithmetic  1.74 us (1%)
    pallas_call x1, Pallas kernels, shards(): pl.pallas_call(functools.partial(kernel, depth), out_shape=(tok_block, to...  139 us

profile of v2, /device:TPU:13, one launch (start us, length us, event | category | flops | bytes accessed | tf_op | source)
XLA Modules:
  0.0 141.4 jit_solution(2828074497360312310)
XLA Ops:
  0.6 0.0 copy-start
  0.6 139.0 %shard_map.113 = (f32[96,512]{1,0:T(8,128)}, f32[96,512]{1,0:T(8,128)}) custom-call(bf16[96,512]{1,0:T(8,128)(2,1)} %q_hbm.1, bf16[96,128]{1,0:T(8,128)(2,1)} %k_hbm.1, bf16[96,128]{1,0:T(8,128)(2,1)} %v_hbm.1, bf16[96,512]{1,0:T(8,128)(2,1)} %res_hbm.1, f32[1,512]{1,0:T(1,128)} %bitcast.13, s32[2,96]{1,0:T(2,128)} %bitcast.14, f32[2,96]{1,0:T(2,128)} %bitcast.15, ...), custom_call_target="tpu_custom_call" | custom-call | tf_op jit(solution)/shard_map/pallas_call | solution.py:640
  139.6 0.0 copy-done
  139.6 1.7 %add_convert_fusion = (bf16[96,512]{1,0:T(8,128)(2,1)}, bf16[96,512]{1,0:T(8,128)(2,1)}) fusion(f32[96,512]{1,0:T(8,128)} %get-tuple-element.5, f32[96,512]{1,0:T(8,128)} %get-tuple-element.4, bf16[96,512]{1,0:T(8,128)(2,1)S(1)} %copy-done), kind=kLoop, calls=%fused_computation | loop fusion | flops 294912 | bytes 688128 | tf_op jit(solution)/shard_map/convert_element_type | solution.py:654
Async XLA Ops:
  0.6 139.0 %copy-start = (bf16[96,512]{1,0:T(8,128)(2,1)S(1)}, bf16[96,512]{1,0:T(8,128)(2,1)}, u32[]{:S(2)}) copy-start(bf16[96,512]{1,0:T(8,128)(2,1)} %res_hbm.1) | copy-start | bytes 294916

commit v3 on v2

--- a/solution.py
+++ b/solution.py
@@ -14,7 +14,7 @@
 TOK = 96
 EXPERTS = 8
 CAP = 36
-PITCH = 48
+PITCH = 40
 PLANE = 4
 ROWS = PLANE * CAP
 WIDE = 512
@@ -220,9 +220,9 @@
     q_hbm, k_hbm, v_hbm, res_hbm, gain_hbm, routes_hbm, gates_hbm, wg_hbm, wu_hbm, wd_hbm,
     attn_out, mix_out,
     q_in, res_in, gain_in, routes_in, gates_in, wg, wu, wd,
-    kvg, qs, m_s, l_s, acc_s, att, ss_buf, outgoing, rx, xg, hb, yb, dr_buf, zr_buf, xr_buf, fb, rb, ret, mixed,
+    kvg, qs, m_s, l_s, acc_s, att, ss_buf, outgoing, rx, xg, hb, yb, dr_buf, zr_buf, xr_buf, fb, rb, ret, mixed, placed, roots,
     load_sem, g_zs, g_xs, g_ds, a_zr, a_xr, a_dr, b_zr, b_xr, b_dr,
-    ss_s, ss_r, x_s, x_r, c_zs, c_zr, c_xs, c_xr, c_ds, c_dr, r_s, r_r,
+    i_zs, i_zr, i_xs, i_xr, i_ds, i_dr, ss_s, ss_r, x_s, x_r, c_zs, c_zr, c_xs, c_xr, c_ds, c_dr, r_s, r_r,
 ):
     p = Place(depth)
     half = p.half
@@ -292,6 +292,7 @@
     slot_ids = lax.broadcasted_iota(jnp.int32, (EXPERTS * PITCH, TOK), 0)
     match = [slot_ids == dest[k] for k in range(2)]
     dispatch = jnp.where(jnp.logical_or(match[0], match[1]), 1.0, 0.0).astype(F32)
+    placed[...] = dispatch
     mixed[...] = jnp.where(match[0], gates_in[0:1, :], 0.0) + jnp.where(match[1], gates_in[1:2, :], 0.0)
 
     scale = 1.0 / math.sqrt(HEAD_WIDTH)
@@ -365,18 +366,7 @@
         cp.start()
         ss_sends.append(cp)
     rows_out = jnp.dot(dispatch.astype(BF16), att[...], preferred_element_type=F32)
-    for i in range(1, n_exp):
-        other = lax.rem(p.exp + n_exp - i, n_exp)
-        remote(ss_buf.at[other], ss_buf.at[other], ss_s.at[i], ss_r.at[i], p.up).wait_recv()
-    total = ss_buf[0, :, pl.ds(0, TOK)]
-    for i in range(1, n_exp):
-        total = total + ss_buf[i, :, pl.ds(0, TOK)]
-    inverse = lax.rsqrt(total / D + 1e-05)
-    columns = lax.dot_general(
-        dispatch, inverse, (((1,), (1,)), ((), ())), precision=lax.Precision.HIGHEST, preferred_element_type=F32
-    )
-    normed = (rows_out * columns[:, 0:1] * gain_in[...]).astype(BF16)
-    outgoing[...] = normed.reshape(EXPERTS, PITCH, WIDE)
+    outgoing[...] = (rows_out * gain_in[...]).astype(BF16).reshape(EXPERTS, PITCH, WIDE)
 
     u_me = lax.rem(p.exp, 2)
     x_sends = []
@@ -395,6 +385,26 @@
 
     kv.finish()
 
+    for i in range(1, n_exp):
+        other = lax.rem(p.exp + n_exp - i, n_exp)
+        remote(ss_buf.at[other], ss_buf.at[other], ss_s.at[i], ss_r.at[i], p.up).wait_recv()
+    total = ss_buf[0, :, pl.ds(0, TOK)]
+    for i in range(1, n_exp):
+        total = total + ss_buf[i, :, pl.ds(0, TOK)]
+    inverse = lax.rsqrt(total / D + 1e-05)
+
+    own_rows = placed[pl.ds(pl.multiple_of(p.exp * PITCH, PITCH), PITCH), :]
+    roots[0, p.j] = jnp.zeros((2, 8, 128), F32)
+    inverse_of = lax.dot_general(
+        inverse, own_rows, (((1,), (1,)), ((), ())), precision=lax.Precision.HIGHEST, preferred_element_type=F32
+    )
+    for part in range(2):
+        roots[0, p.j, part, :, pl.ds(0, PITCH)] = inverse_of
+    iv = KvGather(p, roots, (i_zs, i_zr, i_xs, i_xr, i_ds, i_dr))
+    iv.start()
+
+    iv.arrive(1)
+
     row_ids = lax.broadcasted_iota(jnp.int32, (ROWS, PLANE * PITCH), 0)
     for i in range(1, PLANE):
         row_ids = row_ids + jnp.where(
@@ -426,17 +436,32 @@
     for cp in weight_loads:
         cp.wait()
     ag.start_partner()
+    iv.arrive(2)
+
+    lane_ids = lax.broadcasted_iota(jnp.int32, (ROWS, 128), 1)
+    line_ids = lax.broadcasted_iota(jnp.int32, (ROWS, 128), 0)
+
+    def roots_of(slot):
+        spread = jnp.zeros((ROWS, 128), F32)
+        for jj in range(PLANE):
+            at = jnp.logical_and(line_ids - jj * CAP == lane_ids, lane_ids < CAP)
+            spread = spread + jnp.where(at, roots[slot, jj, 0, 0:1, :], 0.0)
+        return jnp.sum(spread, axis=1, keepdims=True)
 
     def hidden(lo, hi):
         count = hi - lo
+        root = jnp.concatenate([roots_of(slot) for slot in range(lo, hi)], axis=0)
         rows = xg[lo:hi].reshape(count * ROWS, D)
         gate = lax.dot_general(rows, wg[...], (((1,), (1,)), ((), ())), preferred_element_type=F32)
         up = lax.dot_general(rows, wu[...], (((1,), (1,)), ((), ())), preferred_element_type=F32)
+        gate, up = gate * root, up * root
         act = gate / (1.0 + jnp.exp(-gate)) * up
         hb[lo:hi] = act.astype(BF16).reshape(count, ROWS, FF_LOCAL)
 
     def hidden_all(d):
         slots = slots_of(d, half)
+        iv.arrive_other(d)
+        iv.arrive_sibling(slots)
         hidden(slots[0], slots[-1] + 1)
 
     sent = []
@@ -532,6 +557,8 @@
             elif k == 0:
                 ag.arrive_sibling(near)
                 hidden_all(d - 1)
+            elif d + 2 <= half:
+                iv.arrive(d + 2)
 
         ag.arrive(d, between)
     ag.arrive_partner(last)
@@ -587,6 +614,7 @@
     give_back(1)
 
     ag.finish()
+    iv.finish()
     for cp in sent:
         cp.wait_send()
     for cp in ss_sends:
@@ -628,11 +656,12 @@
         vmem((slots, ROWS, D), BF16), vmem((slots, ROWS, FF_LOCAL), BF16), vmem((slots, ROWS, D), BF16),
         vmem((slots, 2, ROWS, 2 * WIDE), BF16), vmem((slots, 3, ROWS, WIDE), BF16), vmem((9, ROWS, WIDE), BF16),
         vmem((2, ROWS, WIDE), BF16), vmem((2, PLANE, PITCH, WIDE), BF16), vmem((EXPERTS, PITCH, WIDE), BF16),
-        vmem((EXPERTS * PITCH, TOK), F32),
+        vmem((EXPERTS * PITCH, TOK), F32), vmem((EXPERTS * PITCH, TOK), F32), vmem((slots, PLANE, 2, 8, 128), F32),
         dma((10,)),
         dma((9, 3)), dma((9,)), dma((8, 4)),
         dma((9, 2)), dma((1,)), dma((8, 2)),
         dma((9, 3)), dma((9,)), dma((8, 4)),
+        dma((9, 2)), dma((9, 2)), dma((1,)), dma((1,)), dma((8, 2)), dma((8, 2)),
         dma((8,)), dma((8,)), dma((8,)), dma((2, PLANE)),
         dma((9, 3)), dma((9, 3)), dma((9,)), dma((9,)), dma((8, 2)), dma((8, 2)),
         dma((8,)), dma((8,)),

time: 141 us -> 140 us (level); the launches traced: 141 us -> 139 us
  Pallas kernels: 139 us -> 136 us
    pallas_call x1, Pallas kernels: 139 us -> 136 us  [shards(): pl.pallas_call(functools.partial(kernel, depth), out_shape=(tok_block, to...]
where the time goes in v3:
time: 140 us; the launch traced here: 139 us
  Pallas kernels  136 us (97%)
  other arithmetic  1.74 us (1%)
    pallas_call x1, Pallas kernels, shards(): pl.pallas_call(functools.partial(kernel, depth), out_shape=(tok_block, to...  136 us

profile of v3, /device:TPU:13, one launch (start us, length us, event | category | flops | bytes accessed | tf_op | source)
XLA Modules:
  0.0 138.7 jit_solution(12512970078655240240)
XLA Ops:
  0.6 0.0 copy-start
  0.6 136.3 %shard_map.113 = (f32[96,512]{1,0:T(8,128)}, f32[96,512]{1,0:T(8,128)}) custom-call(bf16[96,512]{1,0:T(8,128)(2,1)} %q_hbm.1, bf16[96,128]{1,0:T(8,128)(2,1)} %k_hbm.1, bf16[96,128]{1,0:T(8,128)(2,1)} %v_hbm.1, bf16[96,512]{1,0:T(8,128)(2,1)} %res_hbm.1, f32[1,512]{1,0:T(1,128)} %bitcast.13, s32[2,96]{1,0:T(2,128)} %bitcast.14, f32[2,96]{1,0:T(2,128)} %bitcast.15, ...), custom_call_target="tpu_custom_call" | custom-call | tf_op jit(solution)/shard_map/pallas_call | solution.py:669
  136.9 0.0 copy-done
  136.9 1.7 %add_convert_fusion = (bf16[96,512]{1,0:T(8,128)(2,1)}, bf16[96,512]{1,0:T(8,128)(2,1)}) fusion(f32[96,512]{1,0:T(8,128)} %get-tuple-element.5, f32[96,512]{1,0:T(8,128)} %get-tuple-element.4, bf16[96,512]{1,0:T(8,128)(2,1)S(1)} %copy-done), kind=kLoop, calls=%fused_computation | loop fusion | flops 294912 | bytes 688128 | tf_op jit(solution)/shard_map/convert_element_type | solution.py:683
Async XLA Ops:
  0.6 136.3 %copy-start = (bf16[96,512]{1,0:T(8,128)(2,1)S(1)}, bf16[96,512]{1,0:T(8,128)(2,1)}, u32[]{:S(2)}) copy-start(bf16[96,512]{1,0:T(8,128)(2,1)} %res_hbm.1) | copy-start | bytes 294916

commit v4 on v3

--- a/solution.py
+++ b/solution.py
@@ -574,7 +574,7 @@
     for s in last:
         for_partner(s)
     for d in range(half, 0, -1):
-        for k in (0, 2):
+        for k in (2, 0):
             for s in slots_of(d, half):
                 reduce_unit(s, d, k)
         for s in slots_of(d - 1, half):

time: 140 us -> 139 us (level)
  no operation moved by 1% of the time
where the time goes in v4:
time: 139 us; the launch traced here: 138 us
  Pallas kernels  136 us (98%)
  other arithmetic  1.74 us (1%)
    pallas_call x1, Pallas kernels, shards(): pl.pallas_call(functools.partial(kernel, depth), out_shape=(tok_block, to...  136 us

profile of v4, /device:TPU:13, one launch (start us, length us, event | category | flops | bytes accessed | tf_op | source)
XLA Modules:
  0.0 138.3 jit_solution(9133262877442259314)
XLA Ops:
  0.6 0.0 copy-start
  0.6 135.9 %shard_map.113 = (f32[96,512]{1,0:T(8,128)}, f32[96,512]{1,0:T(8,128)}) custom-call(bf16[96,512]{1,0:T(8,128)(2,1)} %q_hbm.1, bf16[96,128]{1,0:T(8,128)(2,1)} %k_hbm.1, bf16[96,128]{1,0:T(8,128)(2,1)} %v_hbm.1, bf16[96,512]{1,0:T(8,128)(2,1)} %res_hbm.1, f32[1,512]{1,0:T(1,128)} %bitcast.13, s32[2,96]{1,0:T(2,128)} %bitcast.14, f32[2,96]{1,0:T(2,128)} %bitcast.15, ...), custom_call_target="tpu_custom_call" | custom-call | tf_op jit(solution)/shard_map/pallas_call | solution.py:669
  136.6 0.0 copy-done
  136.6 1.7 %add_convert_fusion = (bf16[96,512]{1,0:T(8,128)(2,1)}, bf16[96,512]{1,0:T(8,128)(2,1)}) fusion(f32[96,512]{1,0:T(8,128)} %get-tuple-element.5, f32[96,512]{1,0:T(8,128)} %get-tuple-element.4, bf16[96,512]{1,0:T(8,128)(2,1)S(1)} %copy-done), kind=kLoop, calls=%fused_computation | loop fusion | flops 294912 | bytes 688128 | tf_op jit(solution)/shard_map/convert_element_type | solution.py:683
Async XLA Ops:
  0.6 136.0 %copy-start = (bf16[96,512]{1,0:T(8,128)(2,1)S(1)}, bf16[96,512]{1,0:T(8,128)(2,1)}, u32[]{:S(2)}) copy-start(bf16[96,512]{1,0:T(8,128)(2,1)} %res_hbm.1) | copy-start | bytes 294916
